TPU v7x, 32 devices: a whole 2x2x4 slice. The times are simulated.
32 devices in a mesh: row: 4 (over z), col: 4 (over y, x), layer: 2 (over core).
Axes of the slice: x: 2, y: 2, z: 4, core: 2. Of those that a mesh axis runs over, the one named last changes fastest.
Arguments:
- wavefunction: float32 [4096, 4096], P('row', 'col'), may hold values from -0.015625 to 1.515625
- start_block: float32 [4096, 2048], P(('col', 'layer'), 'row'), may hold values from -6 to 6
Outputs:
- basis: float32 [4096, 2048], P(('col', 'layer'), 'row')
All inputs are finite; a program needn't handle non-finite values.
Results may differ from a plain program's by a relative error of at most 0.0003.
Values sent between devices are 32-bit elements; how exact they have to be, the bound alone decides.
No kernel may reach another device: no remote copies, remote signals or barrier semaphores. Data moves between devices by JAX's collectives and lax.ppermute only.
A program may use at most 128 MiB of HBM per device.

v0:
```python
import math
import jax
import jax.numpy as jnp
from jax import lax
from jax.sharding import PartitionSpec as P


def spread(x, axis, root):
    mine = lax.axis_index(axis) == root
    return lax.psum(jnp.where(mine, x, jnp.zeros_like(x)), axis)


def cross(left, right):
    return lax.dot_general(
        left,
        right,
        (((0,), (0,)), ((), ())),
        precision=lax.Precision.HIGHEST,
        preferred_element_type=jnp.float32,
    )


def times(left, right):
    return jnp.dot(left, right, precision=lax.Precision.HIGHEST, preferred_element_type=jnp.float32)


def apply_density(rho_slab, basis_block):
    return lax.psum_scatter(
        cross(rho_slab, basis_block), ("col", "layer"), scatter_dimension=0, tiled=True
    )


def orthonormalize(image_block):
    panel_owner = lax.axis_index("row")
    panels = lax.axis_size("row")
    current = image_block
    gram_matrix = lax.psum(cross(current, current), ("col", "layer"))
    for panel_index in range(panels):
        factor = jnp.linalg.cholesky(gram_matrix)
        new_basis = jax.scipy.linalg.solve_triangular(factor, current.T, lower=True).T
        current = jnp.where(panel_owner == panel_index, new_basis, current)
        if panel_index + 1 < panels:
            chosen = spread(current, "row", panel_index)
            later = panel_owner > panel_index
            correlation, square = lax.psum(
                (cross(chosen, current), cross(current, current)), ("col", "layer")
            )
            current = jnp.where(later, current - times(chosen, correlation), current)
            gram_matrix = jnp.where(later, square - cross(correlation, correlation), square)
    return current


def shards(wavefunction, start_block):
    layers = lax.axis_size("layer")
    column_width = wavefunction.shape[1] // layers
    own_slice = lax.dynamic_slice_in_dim(
        wavefunction, lax.axis_index("layer") * column_width, column_width, 1
    )
    own_rows = lax.all_gather(own_slice, "col", axis=1, tiled=True)
    partner = spread(own_rows, "row", lax.axis_index("col"))
    rho_part = lax.psum_scatter(
        lax.dot_general(
            partner,
            own_rows,
            (((1,), (1,)), ((), ())),
            precision=lax.Precision.HIGHEST,
            preferred_element_type=jnp.float32,
        ),
        "layer",
        scatter_dimension=0,
        tiled=True,
    )
    rho_slab = lax.all_gather(rho_part, "row", axis=1, tiled=True)
    current = start_block
    image_block = apply_density(rho_slab, current)
    current = orthonormalize(image_block)
    return current * math.sqrt(rho_slab.shape[1])


def solution(mesh):
    placed = (P("row", "col"), P(("col", "layer"), "row"))
    return jax.shard_map(
        shards, mesh=mesh, in_specs=placed, out_specs=P(("col", "layer"), "row"), check_vma=False
    )
```

profile of v0, /device:TPU:0, one launch (start us, length us, event | category | flops | bytes accessed | tf_op | source)
XLA Modules:
  0.0 1721.6 jit_solution(5460350467099761118)
XLA Ops:
  9.9 90.3 %all-gather.3.cloned.1.call-done = f32[1024,2048]{1,0:T(8,128)} async-done(((f32[1024,512]{1,0:T(8,128)}), f32[1024,2048]{1,0:T(8,128)}) %all-gather.3.cloned.1.call-update) | async-done | bytes 8388624 | tf_op jit(solution)/shard_map/all_gather | solution.py:59
  108.5 290.9 %all-reduce.13.cloned.1.call-done = f32[1024,2048]{1,0:T(8,128)} async-done(((f32[1024,2048]{1,0:T(8,128)}), f32[1024,2048]{1,0:T(8,128)}) %all-reduce.13.cloned.1.call-update) | async-done | bytes 8388624 | tf_op jit(solution)/shard_map/psum | solution.py:10
  399.4 32.1 %fusion.156 = f32[1024,1024]{1,0:T(8,128)} fusion(f32[1024,2048]{1,0:T(8,128)} %all-reduce.13.cloned.1.call-done, f32[1024,2048]{1,0:T(8,128)} %all-gather.3.cloned.1.call-done), kind=kOutput, calls=%fused_computation.284 | convolution fusion | flops 25769803776 | bytes 20971520 | tf_op jit(solution)/shard_map/dot_general | solution.py:62
  443.1 152.0 %all-gather.5.cloned.1.call-done = f32[512,4096]{1,0:T(8,128)} async-done(((f32[512,1024]{1,0:T(8,128)}), f32[512,4096]{1,0:T(8,128)}) %all-gather.5.cloned.1.call-update) | async-done | bytes 8388624 | tf_op jit(solution)/shard_map/all_gather | solution.py:73
  595.1 17.1 fusion.157
  612.2 69.6 %reduce-scatter.5.cloned.1.call-done = f32[512,512]{0,1:T(8,128)} async-done(((f32[4096,512]{0,1:T(8,128)}), f32[512,512]{0,1:T(8,128)}) %reduce-scatter.5.cloned.1.call-update) | async-done | bytes 1048592 | tf_op jit(solution)/shard_map/reduce_scatter | solution.py:28
  686.9 56.3 %all-reduce.15.cloned.1.call-done = f32[512,512]{0,1:T(8,128)} async-done(((f32[512,512]{0,1:T(8,128)}), f32[512,512]{0,1:T(8,128)}) %all-reduce.15.cloned.1.call-update) | async-done | bytes 1048592 | tf_op jit(solution)/shard_map/psum | solution.py:37
  746.2 11.7 cholesky.462
  768.6 11.7 cholesky.481
  790.9 11.7 cholesky.502
  813.8 11.7 cholesky.519
  838.3 39.3 %custom-call.38 = f32[4,128,128]{1,2,0:T(8,128)S(1)} custom-call(f32[4,128,128]{2,1,0:T(8,128)S(1)} %get-tuple-element.33), custom_call_target="InvertDiagBlocksLowerTriangular" | custom-call | tf_op jit(solution)/shard_map/jit(_solve_triangular)/triangular_solve | solution.py:40
  884.9 48.4 %all-reduce.17.cloned.1.call-done = f32[512,512]{0,1:T(8,128)} async-done(((f32[512,512]{0,1:T(8,128)}), f32[512,512]{0,1:T(8,128)}) %all-reduce.17.cloned.1.call-update) | async-done | bytes 1048592 | tf_op jit(solution)/shard_map/psum | solution.py:10
  937.8 60.8 %all-reduce.27.cloned.1.call-done = (f32[512,512]{1,0:T(8,128)}, f32[512,512]{0,1:T(8,128)}) async-done(((f32[512,512]{1,0:T(8,128)}, f32[512,512]{0,1:T(8,128)}), (f32[512,512]{1,0:T(8,128)}, f32[512,512]{0,1:T(8,128)})) %all-reduce.27.cloned.1.call-update) | async-done | bytes 2097168 | tf_op jit(solution)/shard_map/psum | solution.py:45
  1006.3 11.7 cholesky.534
  1030.6 11.9 cholesky.553
  1055.2 11.7 cholesky.574
  1078.8 12.1 cholesky.591
  1106.6 39.3 %custom-call.42 = f32[4,128,128]{1,2,0:T(8,128)S(1)} custom-call(f32[4,128,128]{2,1,0:T(8,128)S(1)} %get-tuple-element.34), custom_call_target="InvertDiagBlocksLowerTriangular" | custom-call | tf_op jit(solution)/shard_map/jit(_solve_triangular)/triangular_solve | solution.py:40
  1159.0 48.2 %all-reduce.19.cloned.1.call-done = f32[512,512]{0,1:T(8,128)} async-done(((f32[512,512]{0,1:T(8,128)}), f32[512,512]{0,1:T(8,128)}) %all-reduce.19.cloned.1.call-update) | async-done | bytes 1048592 | tf_op jit(solution)/shard_map/psum | solution.py:10
  1211.5 61.1 %all-reduce.25.cloned.1.call-done = (f32[512,512]{1,0:T(8,128)}, f32[512,512]{0,1:T(8,128)}) async-done(((f32[512,512]{1,0:T(8,128)}, f32[512,512]{0,1:T(8,128)}), (f32[512,512]{1,0:T(8,128)}, f32[512,512]{0,1:T(8,128)})) %all-reduce.25.cloned.1.call-update) | async-done | bytes 2097168 | tf_op jit(solution)/shard_map/psum | solution.py:45
  1280.2 11.7 cholesky.606
  1304.5 11.9 cholesky.625
  1329.1 11.7 cholesky.646
  1352.8 12.1 cholesky.663
  1380.5 39.3 %custom-call.46 = f32[4,128,128]{1,2,0:T(8,128)S(1)} custom-call(f32[4,128,128]{2,1,0:T(8,128)S(1)} %get-tuple-element.35), custom_call_target="InvertDiagBlocksLowerTriangular" | custom-call | tf_op jit(solution)/shard_map/jit(_solve_triangular)/triangular_solve | solution.py:40
  1433.1 48.0 %all-reduce.21.cloned.1.call-done = f32[512,512]{0,1:T(8,128)} async-done(((f32[512,512]{0,1:T(8,128)}), f32[512,512]{0,1:T(8,128)}) %all-reduce.21.cloned.1.call-update) | async-done | bytes 1048592 | tf_op jit(solution)/shard_map/psum | solution.py:10
  1485.2 61.3 %all-reduce.23.cloned.1.call-done = (f32[512,512]{1,0:T(8,128)}, f32[512,512]{0,1:T(8,128)}) async-done(((f32[512,512]{1,0:T(8,128)}, f32[512,512]{0,1:T(8,128)}), (f32[512,512]{1,0:T(8,128)}, f32[512,512]{0,1:T(8,128)})) %all-reduce.23.cloned.1.call-update) | async-done | bytes 2097168 | tf_op jit(solution)/shard_map/psum | solution.py:45
  1554.2 11.7 cholesky.678
  1631.5 11.7 cholesky.735
  1650.2 13.7 while.11
  1663.9 40.1 %custom-call.50 = f32[4,128,128]{1,2,0:T(8,128)S(1)} custom-call(f32[4,128,128]{2,1,0:T(8,128)} %get-tuple-element.36), custom_call_target="InvertDiagBlocksLowerTriangular" | custom-call | tf_op jit(solution)/shard_map/jit(_solve_triangular)/triangular_solve | solution.py:40
  (245 shorter events, 368.6 us)
Async XLA Ops:
  6.5 588.5 %copy-start = (f32[512,512]{1,0:T(8,128)S(1)}, f32[512,512]{1,0:T(8,128)}, u32[]{:S(2)}) copy-start(f32[512,512]{1,0:T(8,128)} %param.6) | copy-start | bytes 3145732
  6.5 93.6 %all-gather.3.cloned.1.call-start = ((), (), s32[]{:S(2)}) async-start(), calls=%async_computation.2 | async-start | bytes 10485760 | tf_op jit(solution)/shard_map/all_gather | solution.py:59
  9.8 389.6 %all-reduce.13.cloned.1.call-start = ((), (), s32[]{:S(2)}) async-start(), calls=%async_computation.3 | async-start | bytes 16777216 | tf_op jit(solution)/shard_map/psum | solution.py:10
  108.4 334.3 %reduce-scatter.3.cloned.1.call-start = ((), (), s32[]{:S(2)}) async-start(), calls=%async_computation.4 | async-start | bytes 6291456 | tf_op jit(solution)/shard_map/reduce_scatter | solution.py:61
  431.5 163.5 %all-gather.5.cloned.1.call-start = ((), (), s32[]{:S(2)}) async-start(), calls=%async_computation.5 | async-start | bytes 10485760 | tf_op jit(solution)/shard_map/all_gather | solution.py:73
  442.7 239.1 %reduce-scatter.5.cloned.1.call-start = ((), (), s32[]{:S(2)}) async-start(), calls=%async_computation.6 | async-start | bytes 9437184 | tf_op jit(solution)/shard_map/reduce_scatter | solution.py:28
  612.2 131.0 %all-reduce.15.cloned.1.call-start = ((), (), s32[]{:S(2)}) async-start(), calls=%async_computation.7 | async-start | bytes 2097152 | tf_op jit(solution)/shard_map/psum | solution.py:37
  681.8 195.8 %copy-start.2 = (f32[512,512]{0,1:T(8,128)S(1)}, f32[512,512]{0,1:T(8,128)}, u32[]{:S(2)}) copy-start(f32[512,512]{0,1:T(8,128)} %reduce-scatter.5.cloned.1.call-done) | copy-start | bytes 3145732
  686.3 247.0 %all-reduce.17.cloned.1.call-start = ((), (), s32[]{:S(2)}) async-start(), calls=%async_computation.8 | async-start | bytes 2097152 | tf_op jit(solution)/shard_map/psum | solution.py:10
  882.0 116.7 %all-reduce.27.cloned.1.call-start = ((), (), s32[]{:S(2)}) async-start(), calls=%async_computation.13 | async-start | bytes 4194304 | tf_op jit(solution)/shard_map/psum | solution.py:45
  937.4 269.8 %all-reduce.19.cloned.1.call-start = ((), (), s32[]{:S(2)}) async-start(), calls=%async_computation.9 | async-start | bytes 2097152 | tf_op jit(solution)/shard_map/psum | solution.py:10
  998.7 147.3 %copy-start.4 = (f32[512,512]{1,0:T(8,128)S(1)}, f32[512,512]{1,0:T(8,128)}, u32[]{:S(2)}) copy-start(f32[512,512]{1,0:T(8,128)} %get-tuple-element.73) | copy-start | bytes 3145732
  1005.4 1.0 copy-start.6
  1156.1 116.5 %all-reduce.25.cloned.1.call-start = ((), (), s32[]{:S(2)}) async-start(), calls=%async_computation.12 | async-start | bytes 4194304 | tf_op jit(solution)/shard_map/psum | solution.py:45
  1211.3 269.9 %all-reduce.21.cloned.1.call-start = ((), (), s32[]{:S(2)}) async-start(), calls=%async_computation.10 | async-start | bytes 2097152 | tf_op jit(solution)/shard_map/psum | solution.py:10
  1272.6 147.3 %copy-start.5 = (f32[512,512]{1,0:T(8,128)S(1)}, f32[512,512]{1,0:T(8,128)}, u32[]{:S(2)}) copy-start(f32[512,512]{1,0:T(8,128)} %get-tuple-element.71) | copy-start | bytes 3145732
  1279.3 1.0 copy-start.7
  1430.1 116.5 %all-reduce.23.cloned.1.call-start = ((), (), s32[]{:S(2)}) async-start(), calls=%async_computation.11 | async-start | bytes 4194304 | tf_op jit(solution)/shard_map/psum | solution.py:45
  1546.5 157.5 %copy-start.3 = (f32[512,512]{1,0:T(8,128)S(1)}, f32[512,512]{1,0:T(8,128)}, u32[]{:S(2)}) copy-start(f32[512,512]{1,0:T(8,128)} %get-tuple-element.69) | copy-start | bytes 3145732
  1553.2 1.0 copy-start.8
  1647.0 67.5 %copy-start.1 = (f32[512,512]{1,0:T(8,128)S(1)}, f32[512,512]{1,0:T(8,128)}, u32[]{:S(2)}) copy-start(f32[512,512]{1,0:T(8,128)} %param.6) | copy-start | bytes 3145732
Sparse Core Ops, SparseCore 0:
  9.9 90.1 all-gather.2
  108.5 290.8 all-reduce.12
  431.7 10.9 reduce-scatter.2
  444.1 150.8 all-gather.4
  612.3 69.4 reduce-scatter.4
  686.4 56.6 all-reduce.14
  882.1 51.1 all-reduce.16
  937.5 61.1 all-reduce.26
  1156.2 50.9 all-reduce.18
  1211.4 61.1 all-reduce.24
  1430.2 50.9 all-reduce.20
  1485.3 61.1 all-reduce.22
where the time goes:
time: 1730 us; the launch traced here: 1720 us
  waiting for transfers between devices  998 us (58%)
  other arithmetic  500 us (29%)
  matrix products  136 us (8%)
  local copies, waits for them, and re-layouts  59.8 us (3%)
  between operations  24.6 us (1%)
    psum x4, waiting for transfers between devices, spread(): return lax.psum(jnp.where(mine, x, jnp.zeros_like(x)), axis)  436 us
    another operation x59, other arithmetic, orthonormalize(): factor = jnp.linalg.cholesky(gram_matrix)  319 us
    psum x3, waiting for transfers between devices, orthonormalize(): lax.psum((cross(chosen, current), cross(current, current)), ('col', 'laye...  183 us
    another operation x9, other arithmetic, orthonormalize(): jax.scipy.linalg.solve_triangular(factor, current.T, lower=True)  163 us
    all_gather x1, waiting for transfers between devices, shards(): rho_slab = lax.all_gather(rho_part, 'row', axis=1, tiled=True)  152 us
    all_gather x1, waiting for transfers between devices, shards(): own_rows = lax.all_gather(own_slice, 'col', axis=1, tiled=True)  90.3 us
    reduce_scatter x1, waiting for transfers between devices, apply_density(): lax.psum_scatter(cross(rho_slab, basis_block), ('col', 'layer'), scatter_...  69.6 us
    psum x1, waiting for transfers between devices, orthonormalize(): gram_matrix = lax.psum(cross(current, current), ('col', 'layer'))  56.3 us
  transfers between devices with their start and end apart: 12, of which 12 were waited for; matrix products, arithmetic and copies ran while one was open for 0% of the time, Pallas kernels for 0%

commit v1 on v0

--- a/solution.py
+++ b/solution.py
@@ -42,9 +42,15 @@
         if panel_index + 1 < panels:
             chosen = spread(current, "row", panel_index)
             later = panel_owner > panel_index
-            correlation, square = lax.psum(
-                (cross(chosen, current), cross(current, current)), ("col", "layer")
-            )
+
+            def cut_seats_all(message):
+                mesh_ax = "layer"
+                group_axis = "col"
+                for no in (group_axis, mesh_ax):
+                    message = jax.lax.psum(message, axis_name=no)
+                return message
+
+            correlation, square = cut_seats_all((cross(chosen, current), cross(current, current)))
             current = jnp.where(later, current - times(chosen, correlation), current)
             gram_matrix = jnp.where(later, square - cross(correlation, correlation), square)
     return current

time: 1730 us -> 1830 us (1.058)
  waiting for transfers between devices: 998 us -> 1100 us
    psum x3 -> x6, waiting for transfers between devices: 183 us -> 277 us  [cut_seats_all(): message = jax.lax.psum(message, axis_name=no)]
  transfers between devices with their start and end apart: 12 -> 15, of which waited for: 12 -> 15; matrix products, arithmetic and copies ran while one was open for 0% -> 0% of each run, Pallas kernels for 0% -> 0%
where the time goes in v1:
time: 1830 us; the launch traced here: 1820 us
  waiting for transfers between devices  1100 us (60%)
  other arithmetic  500 us (27%)
  matrix products  137 us (7%)
  local copies, waits for them, and re-layouts  59.8 us (3%)
  between operations  24.6 us (1%)
    psum x4, waiting for transfers between devices, spread(): return lax.psum(jnp.where(mine, x, jnp.zeros_like(x)), axis)  440 us
    another operation x59, other arithmetic, orthonormalize(): factor = jnp.linalg.cholesky(gram_matrix)  319 us
    psum x6, waiting for transfers between devices, cut_seats_all(): message = jax.lax.psum(message, axis_name=no)  277 us
    another operation x9, other arithmetic, orthonormalize(): jax.scipy.linalg.solve_triangular(factor, current.T, lower=True)  163 us
    all_gather x1, waiting for transfers between devices, shards(): rho_slab = lax.all_gather(rho_part, 'row', axis=1, tiled=True)  152 us
    all_gather x1, waiting for transfers between devices, shards(): own_rows = lax.all_gather(own_slice, 'col', axis=1, tiled=True)  90.3 us
    reduce_scatter x1, waiting for transfers between devices, apply_density(): lax.psum_scatter(cross(rho_slab, basis_block), ('col', 'layer'), scatter_...  69.6 us
    psum x1, waiting for transfers between devices, orthonormalize(): gram_matrix = lax.psum(cross(current, current), ('col', 'layer'))  56.6 us
  transfers between devices with their start and end apart: 15, of which 15 were waited for; matrix products, arithmetic and copies ran while one was open for 0% of the time, Pallas kernels for 0%

profile of v1, /device:TPU:0, one launch (start us, length us, event | category | flops | bytes accessed | tf_op | source)
XLA Modules:
  0.0 1819.7 jit_solution(1168757772040982731)
XLA Ops:
  9.9 90.3 %all-gather.3.cloned.1.call-done = f32[1024,2048]{1,0:T(8,128)} async-done(((f32[1024,512]{1,0:T(8,128)}), f32[1024,2048]{1,0:T(8,128)}) %all-gather.3.cloned.1.call-update) | async-done | bytes 8388624 | tf_op jit(solution)/shard_map/all_gather | solution.py:65
  108.5 290.9 %all-reduce.19.cloned.1.call-done = f32[1024,2048]{1,0:T(8,128)} async-done(((f32[1024,2048]{1,0:T(8,128)}), f32[1024,2048]{1,0:T(8,128)}) %all-reduce.19.cloned.1.call-update) | async-done | bytes 8388624 | tf_op jit(solution)/shard_map/psum | solution.py:10
  399.4 32.1 %fusion.156 = f32[1024,1024]{1,0:T(8,128)} fusion(f32[1024,2048]{1,0:T(8,128)} %all-reduce.19.cloned.1.call-done, f32[1024,2048]{1,0:T(8,128)} %all-gather.3.cloned.1.call-done), kind=kOutput, calls=%fused_computation.284 | convolution fusion | flops 25769803776 | bytes 20971520 | tf_op jit(solution)/shard_map/dot_general | solution.py:68
  443.0 152.1 %all-gather.5.cloned.1.call-done = f32[512,4096]{1,0:T(8,128)} async-done(((f32[512,1024]{1,0:T(8,128)}), f32[512,4096]{1,0:T(8,128)}) %all-gather.5.cloned.1.call-update) | async-done | bytes 8388624 | tf_op jit(solution)/shard_map/all_gather | solution.py:79
  595.1 17.1 fusion.157
  612.2 69.6 %reduce-scatter.5.cloned.1.call-done = f32[512,512]{0,1:T(8,128)} async-done(((f32[4096,512]{0,1:T(8,128)}), f32[512,512]{0,1:T(8,128)}) %reduce-scatter.5.cloned.1.call-update) | async-done | bytes 1048592 | tf_op jit(solution)/shard_map/reduce_scatter | solution.py:28
  686.6 56.6 %all-reduce.21.cloned.1.call-done = f32[512,512]{0,1:T(8,128)} async-done(((f32[512,512]{0,1:T(8,128)}), f32[512,512]{0,1:T(8,128)}) %all-reduce.21.cloned.1.call-update) | async-done | bytes 1048592 | tf_op jit(solution)/shard_map/psum | solution.py:37
  746.2 11.7 cholesky.462
  768.6 11.7 cholesky.481
  791.2 11.7 cholesky.502
  814.1 11.7 cholesky.519
  838.5 39.3 %custom-call.38 = f32[4,128,128]{1,2,0:T(8,128)S(1)} custom-call(f32[4,128,128]{2,1,0:T(8,128)S(1)} %get-tuple-element.33), custom_call_target="InvertDiagBlocksLowerTriangular" | custom-call | tf_op jit(solution)/shard_map/jit(_solve_triangular)/triangular_solve | solution.py:40
  885.2 48.3 %all-reduce.23.cloned.1.call-done = f32[512,512]{0,1:T(8,128)} async-done(((f32[512,512]{0,1:T(8,128)}), f32[512,512]{0,1:T(8,128)}) %all-reduce.23.cloned.1.call-update) | async-done | bytes 1048592 | tf_op jit(solution)/shard_map/psum | solution.py:10
  937.7 68.9 %all-reduce.33.cloned.1.call-done = (f32[512,512]{1,0:T(8,128)}, f32[512,512]{0,1:T(8,128)}) async-done(((f32[512,512]{1,0:T(8,128)}, f32[512,512]{0,1:T(8,128)}), (f32[512,512]{1,0:T(8,128)}, f32[512,512]{0,1:T(8,128)})) %all-reduce.33.cloned.1.call-update) | async-done | bytes 2097168 | tf_op jit(solution)/shard_map/psum | solution.py:50
  1006.8 23.5 %all-reduce.39.cloned.1.call-done = (f32[512,512]{1,0:T(8,128)}, f32[512,512]{0,1:T(8,128)}) async-done(((f32[512,512]{1,0:T(8,128)}, f32[512,512]{0,1:T(8,128)}), (f32[512,512]{1,0:T(8,128)}, f32[512,512]{0,1:T(8,128)})) %all-reduce.39.cloned.1.call-update) | async-done | bytes 2097168 | tf_op jit(solution)/shard_map/psum | solution.py:50
  1038.0 11.7 cholesky.534
  1062.2 12.2 cholesky.553
  1110.8 11.9 cholesky.591
  1138.3 39.3 %custom-call.42 = f32[4,128,128]{1,2,0:T(8,128)S(1)} custom-call(f32[4,128,128]{2,1,0:T(8,128)S(1)} %get-tuple-element.34), custom_call_target="InvertDiagBlocksLowerTriangular" | custom-call | tf_op jit(solution)/shard_map/jit(_solve_triangular)/triangular_solve | solution.py:40
  1190.8 50.3 %all-reduce.25.cloned.1.call-done = f32[512,512]{0,1:T(8,128)} async-done(((f32[512,512]{0,1:T(8,128)}), f32[512,512]{0,1:T(8,128)}) %all-reduce.25.cloned.1.call-update) | async-done | bytes 1048592 | tf_op jit(solution)/shard_map/psum | solution.py:10
  1245.2 68.9 %all-reduce.31.cloned.1.call-done = (f32[512,512]{1,0:T(8,128)}, f32[512,512]{0,1:T(8,128)}) async-done(((f32[512,512]{1,0:T(8,128)}, f32[512,512]{0,1:T(8,128)}), (f32[512,512]{1,0:T(8,128)}, f32[512,512]{0,1:T(8,128)})) %all-reduce.31.cloned.1.call-update) | async-done | bytes 2097168 | tf_op jit(solution)/shard_map/psum | solution.py:50
  1314.5 23.2 %all-reduce.37.cloned.1.call-done = (f32[512,512]{1,0:T(8,128)}, f32[512,512]{0,1:T(8,128)}) async-done(((f32[512,512]{1,0:T(8,128)}, f32[512,512]{0,1:T(8,128)}), (f32[512,512]{1,0:T(8,128)}, f32[512,512]{0,1:T(8,128)})) %all-reduce.37.cloned.1.call-update) | async-done | bytes 2097168 | tf_op jit(solution)/shard_map/psum | solution.py:50
  1369.6 11.9 cholesky.625
  1417.9 12.1 cholesky.663
  1445.7 39.3 %custom-call.46 = f32[4,128,128]{1,2,0:T(8,128)S(1)} custom-call(f32[4,128,128]{2,1,0:T(8,128)S(1)} %get-tuple-element.35), custom_call_target="InvertDiagBlocksLowerTriangular" | custom-call | tf_op jit(solution)/shard_map/jit(_solve_triangular)/triangular_solve | solution.py:40
  1498.1 50.3 %all-reduce.27.cloned.1.call-done = f32[512,512]{0,1:T(8,128)} async-done(((f32[512,512]{0,1:T(8,128)}), f32[512,512]{0,1:T(8,128)}) %all-reduce.27.cloned.1.call-update) | async-done | bytes 1048592 | tf_op jit(solution)/shard_map/psum | solution.py:10
  1552.7 68.7 %all-reduce.29.cloned.1.call-done = (f32[512,512]{1,0:T(8,128)}, f32[512,512]{0,1:T(8,128)}) async-done(((f32[512,512]{1,0:T(8,128)}, f32[512,512]{0,1:T(8,128)}), (f32[512,512]{1,0:T(8,128)}, f32[512,512]{0,1:T(8,128)})) %all-reduce.29.cloned.1.call-update) | async-done | bytes 2097168 | tf_op jit(solution)/shard_map/psum | solution.py:50
  1621.4 23.6 %all-reduce.35.cloned.1.call-done = (f32[512,512]{1,0:T(8,128)}, f32[512,512]{0,1:T(8,128)}) async-done(((f32[512,512]{1,0:T(8,128)}, f32[512,512]{0,1:T(8,128)}), (f32[512,512]{1,0:T(8,128)}, f32[512,512]{0,1:T(8,128)})) %all-reduce.35.cloned.1.call-update) | async-done | bytes 2097168 | tf_op jit(solution)/shard_map/psum | solution.py:50
  1678.6 11.9 cholesky.697
  1729.7 11.9 cholesky.735
  1748.6 13.5 while.11
  1762.1 40.1 %custom-call.50 = f32[4,128,128]{1,2,0:T(8,128)S(1)} custom-call(f32[4,128,128]{2,1,0:T(8,128)} %get-tuple-element.36), custom_call_target="InvertDiagBlocksLowerTriangular" | custom-call | tf_op jit(solution)/shard_map/jit(_solve_triangular)/triangular_solve | solution.py:40
  (254 shorter events, 403.3 us)
Async XLA Ops:
  6.5 588.5 %copy-start = (f32[512,512]{1,0:T(8,128)S(1)}, f32[512,512]{1,0:T(8,128)}, u32[]{:S(2)}) copy-start(f32[512,512]{1,0:T(8,128)} %param.6) | copy-start | bytes 3145732
  6.5 93.6 %all-gather.3.cloned.1.call-start = ((), (), s32[]{:S(2)}) async-start(), calls=%async_computation.2 | async-start | bytes 10485760 | tf_op jit(solution)/shard_map/all_gather | solution.py:65
  9.8 389.6 %all-reduce.19.cloned.1.call-start = ((), (), s32[]{:S(2)}) async-start(), calls=%async_computation.3 | async-start | bytes 16777216 | tf_op jit(solution)/shard_map/psum | solution.py:10
  108.4 334.3 %reduce-scatter.3.cloned.1.call-start = ((), (), s32[]{:S(2)}) async-start(), calls=%async_computation.4 | async-start | bytes 6291456 | tf_op jit(solution)/shard_map/reduce_scatter | solution.py:67
  431.5 163.5 %all-gather.5.cloned.1.call-start = ((), (), s32[]{:S(2)}) async-start(), calls=%async_computation.5 | async-start | bytes 10485760 | tf_op jit(solution)/shard_map/all_gather | solution.py:79
  442.7 239.1 %reduce-scatter.5.cloned.1.call-start = ((), (), s32[]{:S(2)}) async-start(), calls=%async_computation.6 | async-start | bytes 9437184 | tf_op jit(solution)/shard_map/reduce_scatter | solution.py:28
  612.2 131.0 %all-reduce.21.cloned.1.call-start = ((), (), s32[]{:S(2)}) async-start(), calls=%async_computation.7 | async-start | bytes 2097152 | tf_op jit(solution)/shard_map/psum | solution.py:37
  681.8 196.0 %copy-start.2 = (f32[512,512]{0,1:T(8,128)S(1)}, f32[512,512]{0,1:T(8,128)}, u32[]{:S(2)}) copy-start(f32[512,512]{0,1:T(8,128)} %reduce-scatter.5.cloned.1.call-done) | copy-start | bytes 3145732
  686.3 247.2 %all-reduce.23.cloned.1.call-start = ((), (), s32[]{:S(2)}) async-start(), calls=%async_computation.8 | async-start | bytes 2097152 | tf_op jit(solution)/shard_map/psum | solution.py:10
  882.2 124.3 %all-reduce.33.cloned.1.call-start = ((), (), s32[]{:S(2)}) async-start(), calls=%async_computation.13 | async-start | bytes 4194304 | tf_op jit(solution)/shard_map/psum | solution.py:50
  937.6 92.7 %all-reduce.39.cloned.1.call-start = ((), (), s32[]{:S(2)}) async-start(), calls=%async_computation.16 | async-start | bytes 4194304 | tf_op jit(solution)/shard_map/psum | solution.py:50
  1006.5 234.5 %all-reduce.25.cloned.1.call-start = ((), (), s32[]{:S(2)}) async-start(), calls=%async_computation.9 | async-start | bytes 2097152 | tf_op jit(solution)/shard_map/psum | solution.py:10
  1030.3 147.3 %copy-start.4 = (f32[512,512]{1,0:T(8,128)S(1)}, f32[512,512]{1,0:T(8,128)}, u32[]{:S(2)}) copy-start(f32[512,512]{1,0:T(8,128)} %get-tuple-element.79) | copy-start | bytes 3145732
  1037.0 1.0 copy-start.6
  1187.8 126.2 %all-reduce.31.cloned.1.call-start = ((), (), s32[]{:S(2)}) async-start(), calls=%async_computation.12 | async-start | bytes 4194304 | tf_op jit(solution)/shard_map/psum | solution.py:50
  1245.1 92.6 %all-reduce.37.cloned.1.call-start = ((), (), s32[]{:S(2)}) async-start(), calls=%async_computation.15 | async-start | bytes 4194304 | tf_op jit(solution)/shard_map/psum | solution.py:50
  1314.1 234.3 %all-reduce.27.cloned.1.call-start = ((), (), s32[]{:S(2)}) async-start(), calls=%async_computation.10 | async-start | bytes 2097152 | tf_op jit(solution)/shard_map/psum | solution.py:10
  1337.7 147.3 %copy-start.5 = (f32[512,512]{1,0:T(8,128)S(1)}, f32[512,512]{1,0:T(8,128)}, u32[]{:S(2)}) copy-start(f32[512,512]{1,0:T(8,128)} %get-tuple-element.77) | copy-start | bytes 3145732
  1344.4 1.0 copy-start.7
  1495.2 126.2 %all-reduce.29.cloned.1.call-start = ((), (), s32[]{:S(2)}) async-start(), calls=%async_computation.11 | async-start | bytes 4194304 | tf_op jit(solution)/shard_map/psum | solution.py:50
  1552.5 92.6 %all-reduce.35.cloned.1.call-start = ((), (), s32[]{:S(2)}) async-start(), calls=%async_computation.14 | async-start | bytes 4194304 | tf_op jit(solution)/shard_map/psum | solution.py:50
  1645.0 157.2 %copy-start.3 = (f32[512,512]{1,0:T(8,128)S(1)}, f32[512,512]{1,0:T(8,128)}, u32[]{:S(2)}) copy-start(f32[512,512]{1,0:T(8,128)} %get-tuple-element.75) | copy-start | bytes 3145732
  1651.7 1.0 copy-start.8
  1745.4 67.4 %copy-start.1 = (f32[512,512]{1,0:T(8,128)S(1)}, f32[512,512]{1,0:T(8,128)}, u32[]{:S(2)}) copy-start(f32[512,512]{1,0:T(8,128)} %param.6) | copy-start | bytes 3145732
Sparse Core Ops, SparseCore 0:
  9.9 90.1 all-gather.2
  108.5 290.8 all-reduce.18
  431.7 10.9 reduce-scatter.2
  444.1 150.8 all-gather.4
  612.3 69.4 reduce-scatter.4
  686.5 56.7 all-reduce.20
  882.4 51.1 all-reduce.22
  937.7 68.7 all-reduce.32
  1008.9 21.3 all-reduce.38
  1188.0 53.0 all-reduce.24
  1245.3 68.7 all-reduce.30
  1316.3 21.3 all-reduce.36
  1495.3 53.0 all-reduce.26
  1552.6 68.7 all-reduce.28
  1623.6 21.3 all-reduce.34
